TPU v7x, 32 devices: a whole 2x2x4 slice. The times are simulated.
32 devices in a mesh: section: 2 (over y), mp: 16 (over z, x, core).
Axes of the slice: x: 2, y: 2, z: 4, core: 2. Of those that a mesh axis runs over, the one named last changes fastest.
Arguments:
- features: bfloat16 [4, 32, 8192], P(None, None, 'mp'), may hold values from -6 to 6
- labels: int32 [4, 32], replicated, may hold values 0 or 1
- weights: bfloat16 [2, 8192, 8192], P('section', None, 'mp'), may hold values from -1.78986404 to 1.78986404
- vectors: float32 [2, 8192], P('section', 'mp'), may hold values from -6 to 6
- head_weight: float32 [8192], P('mp'), may hold values from -0.0625 to 0.0625
Outputs:
- weight_grad: bfloat16 [2, 8192, 8192], P('section', None, 'mp')
- new_vectors: float32 [2, 8192], P('section', 'mp')
- rank_coef: float32 [2], P('section')
All inputs are finite; a program needn't handle non-finite values.
Results may differ from a plain program's by a relative error of at most 0.015.
Values may be sent and summed in bfloat16 or wider, within the bound.
No kernel may reach another device: no remote copies, remote signals or barrier semaphores. Data moves between devices by JAX's collectives and lax.ppermute only.
A program may use at most 64 MiB of HBM per device.

v0:
```python
import jax
import jax.numpy as jnp
from jax import lax
from jax.sharding import PartitionSpec as P

loss_scale = 32.0
tiny_eps = 1e-06


def shifted(block, axis, distance):
    devices = range(lax.axis_size(axis))
    route = [(i - distance, i) for i in devices if i - distance in devices]
    return lax.ppermute(block, axis, route)


def silu_slope(pre_act):
    gate_val = jax.nn.sigmoid(pre_act)
    return gate_val * (1.0 + pre_act * (1.0 - gate_val))


def keep_slot(stored, update, micro_slot, is_live):
    previous = lax.dynamic_index_in_dim(stored, micro_slot, 0, keepdims=False)
    return lax.dynamic_update_index_in_dim(
        stored, jnp.where(is_live, update, previous), micro_slot, 0
    )


def power_step(weight, vector_u):
    vector_bf = vector_u.astype(jnp.bfloat16)
    left_sum = lax.psum(jnp.dot(weight, vector_bf, preferred_element_type=jnp.float32), "mp")
    vector_v = (left_sum * lax.rsqrt(jnp.sum(left_sum * left_sum) + tiny_eps)).astype(jnp.bfloat16)
    right_part = jnp.dot(vector_v, weight, preferred_element_type=jnp.float32)
    norm_total = lax.psum(jnp.sum(right_part * right_part), "mp")
    spectral = jnp.sqrt(norm_total + tiny_eps)
    return (spectral, right_part / spectral)


def on_device(features, labels, weights, vectors, head_weight):
    weight = weights[0]
    vector_u = vectors[0]
    micro_count, batch_rows, local_cols = features.shape
    full_width = weight.shape[0]
    sections = lax.axis_size("section")
    section_index = lax.axis_index("section")
    tick_count = micro_count + sections - 1
    sign_all = (2 * labels - 1).astype(jnp.float32)
    spectral_init, new_init = power_step(weight, vector_u)

    def forward_tick(tick_now, state_all):
        incoming, inputs_all, pre_all, logits_all, spectral, new_u = state_all
        micro_index = tick_now - section_index
        is_live = (micro_index >= 0) & (micro_index < micro_count)
        micro_slot = jnp.clip(micro_index, 0, micro_count - 1)
        first_input = lax.dynamic_index_in_dim(features, micro_slot, 0, keepdims=False)
        layer_in = jnp.where(section_index == 0, first_input, incoming)
        shard_piece = lax.all_gather(layer_in, "mp", axis=1, tiled=True)
        accum_part = jnp.dot(shard_piece, weight, preferred_element_type=jnp.float32)
        whole_rows = shard_piece
        accum_part, whole_rows = (accum_part, whole_rows)
        pre_act = accum_part / spectral
        layer_out = (layer_in.astype(jnp.float32) + jax.nn.silu(pre_act)).astype(jnp.bfloat16)
        partial_logit = jnp.sum(layer_out.astype(jnp.float32) * head_weight[None, :], axis=1)
        inputs_all = keep_slot(inputs_all, whole_rows, micro_slot, is_live)
        pre_all = keep_slot(pre_all, pre_act, micro_slot, is_live)
        logits_all = keep_slot(
            logits_all, partial_logit, micro_slot, is_live & (section_index == sections - 1)
        )
        incoming = shifted(layer_out, "section", 1)
        return (incoming, inputs_all, pre_all, logits_all, spectral, new_u)

    start_state = (
        jnp.zeros((batch_rows, local_cols), jnp.bfloat16),
        jnp.zeros((micro_count, batch_rows, full_width), jnp.bfloat16),
        jnp.zeros((micro_count, batch_rows, local_cols), jnp.float32),
        jnp.zeros((micro_count, batch_rows), jnp.float32),
        spectral_init,
        new_init,
    )
    _, inputs_all, pre_all, partial_logits, spectral, new_u = lax.fori_loop(
        0, tick_count, forward_tick, start_state
    )
    logits_all = lax.psum(partial_logits, "mp")

    def backward_tick(tick_now, state_all):
        incoming, grad_all = state_all
        micro_index = tick_now - (sections - 1 - section_index)
        is_live = (micro_index >= 0) & (micro_index < micro_count)
        micro_slot = jnp.clip(micro_index, 0, micro_count - 1)
        sign_row = lax.dynamic_index_in_dim(sign_all, micro_slot, 0, keepdims=False)
        logit_row = lax.dynamic_index_in_dim(logits_all, micro_slot, 0, keepdims=False)
        top_scale = -loss_scale * sign_row * jax.nn.sigmoid(-sign_row * logit_row)
        top_grad = (top_scale[:, None] * head_weight[None, :]).astype(jnp.bfloat16)
        grad_out = jnp.where(section_index == sections - 1, top_grad, incoming)
        pre_act = lax.dynamic_index_in_dim(pre_all, micro_slot, 0, keepdims=False)
        grad_pre = (grad_out.astype(jnp.float32) * silu_slope(pre_act)).astype(jnp.bfloat16)
        partial_term = lax.dot_general(
            grad_pre, weight, (((1,), (1,)), ((), ())), preferred_element_type=jnp.float32
        )
        received = lax.all_to_all(
            partial_term.astype(jnp.bfloat16), "mp", split_axis=1, concat_axis=0, tiled=True
        ).astype(partial_term.dtype)
        back_sum = jnp.sum(received.reshape(-1, batch_rows, local_cols), axis=0)
        grad_in = (grad_out.astype(jnp.float32) + back_sum / spectral).astype(jnp.bfloat16)
        grad_all = keep_slot(grad_all, grad_pre, micro_slot, is_live)
        incoming = shifted(grad_in, "section", -1)
        return (incoming, grad_all)

    back_state = (
        jnp.zeros((batch_rows, local_cols), jnp.bfloat16),
        jnp.zeros((micro_count, batch_rows, local_cols), jnp.bfloat16),
    )
    _, grad_all = lax.fori_loop(0, tick_count, backward_tick, back_state)
    whole_rows = inputs_all.reshape(micro_count * batch_rows, full_width)
    grad_rows = grad_all.reshape(micro_count * batch_rows, local_cols)
    outer_sum = lax.dot_general(
        whole_rows, grad_rows, (((0,), (0,)), ((), ())), preferred_element_type=jnp.float32
    )
    weight_grad = (outer_sum / spectral).astype(jnp.bfloat16)
    inner_total = lax.psum(jnp.sum(outer_sum * weight.astype(jnp.float32)), "mp")
    rank_coef = inner_total / (spectral * spectral)
    return (weight_grad[None], new_u[None], rank_coef.reshape(1))


def solution(mesh):
    placed = (P(None, None, "mp"), P(), P("section", None, "mp"), P("section", "mp"), P("mp"))
    return jax.shard_map(
        on_device,
        mesh=mesh,
        in_specs=placed,
        out_specs=(P("section", None, "mp"), P("section", "mp"), P("section")),
        check_vma=False,
    )
```

profile of v0, /device:TPU:0, one launch (start us, length us, event | category | flops | bytes accessed | tf_op | source)
XLA Modules:
  0.0 495.4 jit_solution(9324954132209440340)
XLA Ops:
  6.3 63.0 %psum.28 = f32[8192]{0:T(1024)S(1)} all-reduce(f32[8192]{0:T(1024)S(1)} %bitcast.113), channel_id=1, replica_groups=mesh['section'=2,'mp'=16] {'mp'}, use_global_device_ids=true, to_apply=%region_0.0 | all-reduce | flops 8192 | bytes 65536 | tf_op jit(solution)/shard_map/psum | solution.py:30
  75.8 30.1 %psum.29 = f32[]{:T(128)} all-reduce(f32[]{:T(128)} %multiply_reduce_fusion.2), channel_id=1, replica_groups=mesh['section'=2,'mp'=16] {'mp'}, use_global_device_ids=true, to_apply=%region_3.0 | all-reduce | flops 1 | bytes 8 | tf_op jit(solution)/shard_map/psum | solution.py:33
  107.4 158.8 %while.37 = (s32[]{:T(128)}, bf16[32,512]{1,0:T(8,128)(2,1)}, bf16[4,32,8192]{2,1,0:T(8,128)(2,1)S(1)}, f32[4,32,512]{2,1,0:T(8,128)S(1)}, f32[4,32]{1,0:T(4,128...) while((s32[]{:T(128)}, bf16[32,512]{1,0:T(8,128)(2,1)}, ...), condition=%wide.region_6.7_spmd, body=%wide.region_4.6_spmd.sunk | while | flops 268910592 | bytes 12782621 | solution.py:79
  108.2 18.7 %all_gather.9 = bf16[32,8192]{1,0:T(8,128)(2,1)S(1)} all-gather(bf16[32,512]{1,0:T(8,128)(2,1)S(1)} %bitcast_select_fusion.5), channel_id=1, replica_groups=mesh['section'=2,'mp'=16] {'mp'}, dimensions={1}, use_global_device_ids=true | all-gather | bytes 557056 | tf_op jit(solution)/shard_map/while/body/eval_jaxpr/all_gather | solution.py:56
  126.9 5.7 %multiply_reduce_fusion.4 = (f32[32]{0:T(128)S(1)}, bf16[32,512]{1,0:T(8,128)(2,1)}, f32[32,512]{1,0:T(8,128)S(1)}) fusion(f32[512]{0:T(512)S(1)} %get-tuple-element.704, bf16[32,512]{1,0:T(8,128)(2,1)S(1)} %bitcast_select_fusion.5, f32[]{:T(128)} %get-tuple-element.702, bf16[32,8192]{1,0:T(8,128)(2,1)S(1)} %all_gather.9, ...), kind=kOutput, calls=%fused_computation.5.clone.1 | convolution fusion | flops 268615648 | bytes 9046148 | tf_op jit(solution)/shard_map/while/body/eval_jaxpr/dot_general | solution.py:57
  138.6 20.4 %all_gather.9 = bf16[32,8192]{1,0:T(8,128)(2,1)S(1)} all-gather(bf16[32,512]{1,0:T(8,128)(2,1)S(1)} %bitcast_select_fusion.5), channel_id=1, replica_groups=mesh['section'=2,'mp'=16] {'mp'}, dimensions={1}, use_global_device_ids=true | all-gather | bytes 557056 | tf_op jit(solution)/shard_map/while/body/eval_jaxpr/all_gather | solution.py:56
  171.6 18.7 %all_gather.9 = bf16[32,8192]{1,0:T(8,128)(2,1)S(1)} all-gather(bf16[32,512]{1,0:T(8,128)(2,1)S(1)} %bitcast_select_fusion.5), channel_id=1, replica_groups=mesh['section'=2,'mp'=16] {'mp'}, dimensions={1}, use_global_device_ids=true | all-gather | bytes 557056 | tf_op jit(solution)/shard_map/while/body/eval_jaxpr/all_gather | solution.py:56
  190.3 5.7 %multiply_reduce_fusion.4 = (f32[32]{0:T(128)S(1)}, bf16[32,512]{1,0:T(8,128)(2,1)}, f32[32,512]{1,0:T(8,128)S(1)}) fusion(f32[512]{0:T(512)S(1)} %get-tuple-element.704, bf16[32,512]{1,0:T(8,128)(2,1)S(1)} %bitcast_select_fusion.5, f32[]{:T(128)} %get-tuple-element.702, bf16[32,8192]{1,0:T(8,128)(2,1)S(1)} %all_gather.9, ...), kind=kOutput, calls=%fused_computation.5.clone.1 | convolution fusion | flops 268615648 | bytes 9046148 | tf_op jit(solution)/shard_map/while/body/eval_jaxpr/dot_general | solution.py:57
  202.8 20.4 %all_gather.9 = bf16[32,8192]{1,0:T(8,128)(2,1)S(1)} all-gather(bf16[32,512]{1,0:T(8,128)(2,1)S(1)} %bitcast_select_fusion.5), channel_id=1, replica_groups=mesh['section'=2,'mp'=16] {'mp'}, dimensions={1}, use_global_device_ids=true | all-gather | bytes 557056 | tf_op jit(solution)/shard_map/while/body/eval_jaxpr/all_gather | solution.py:56
  235.8 18.7 %all_gather.9 = bf16[32,8192]{1,0:T(8,128)(2,1)S(1)} all-gather(bf16[32,512]{1,0:T(8,128)(2,1)S(1)} %bitcast_select_fusion.5), channel_id=1, replica_groups=mesh['section'=2,'mp'=16] {'mp'}, dimensions={1}, use_global_device_ids=true | all-gather | bytes 557056 | tf_op jit(solution)/shard_map/while/body/eval_jaxpr/all_gather | solution.py:56
  266.2 30.4 %psum.30 = f32[4,32]{1,0:T(4,128)S(1)} all-reduce(f32[4,32]{1,0:T(4,128)S(1)} %get-tuple-element.461), channel_id=1, replica_groups=mesh['section'=2,'mp'=16] {'mp'}, use_global_device_ids=true, to_apply=%region_7.8 | all-reduce | flops 128 | bytes 1024 | tf_op jit(solution)/shard_map/psum | solution.py:82
  297.4 155.4 %while.38 = (s32[]{:T(128)}, bf16[32,512]{1,0:T(8,128)(2,1)S(1)}, bf16[4,32,512]{2,1,0:T(8,128)(2,1)S(1)}, pred[]{:T(512)}, s32[]{:T(128)}, /*index=5*/f32[4,32]...) while((s32[]{:T(128)}, bf16[32,512]{1,0:T(8,128)(2,1)S(1)}, ...), condition=%wide.region_10.11_spmd, body=%wide.region_8.10_spmd.sunk | while | flops 269762784 | bytes 12787494 | solution.py:112
  297.4 5.9 %convolution_convert_fusion.2 = bf16[32,8192]{1,0:T(8,128)(2,1)S(1)} fusion(bf16[8192,512]{1,0:T(8,128)(2,1)} %get-tuple-element.748, f32[4,32,512]{2,1,0:T(8,128)S(1)} %get-tuple-element.747, s32[]{:T(128)S(6)} %min.21, bf16[32,512]{1,0:T(8,128)(2,1)S(1)} %get-tuple-element.725, f32[512]{0:T(512)S(1)} %get-tuple-element.746, f32[32]{0:T(128)S(1)} %fusion.37, ...), kind=kOutput, calls=%fused_computation.12.clone.1 | convolution fusion | flops 268910592 | bytes 9013765 | tf_op jit(solution)/shard_map/while/body/eval_jaxpr/dot_general | solution.py:96
  307.8 14.2 %all-to-all-done = bf16[32,16,512]{2,0,1:T(8,128)(2,1)S(1)} async-done(((bf16[32,16,512]{2,0,1:T(8,128)(2,1)}), bf16[32,16,512]{2,0,1:T(8,128)(2,1)S(1)}, u32[]{:S(2)}, u32[]{:S(2)}) %all-to-all-start) | async-done | bytes 524320 | tf_op jit(solution)/shard_map/while/body/eval_jaxpr/all_to_all | solution.py:99
  328.0 5.9 %convolution_convert_fusion.2 = bf16[32,8192]{1,0:T(8,128)(2,1)S(1)} fusion(bf16[8192,512]{1,0:T(8,128)(2,1)} %get-tuple-element.748, f32[4,32,512]{2,1,0:T(8,128)S(1)} %get-tuple-element.747, s32[]{:T(128)S(6)} %min.21, bf16[32,512]{1,0:T(8,128)(2,1)S(1)} %get-tuple-element.725, f32[512]{0:T(512)S(1)} %get-tuple-element.746, f32[32]{0:T(128)S(1)} %fusion.37, ...), kind=kOutput, calls=%fused_computation.12.clone.1 | convolution fusion | flops 268910592 | bytes 9013765 | tf_op jit(solution)/shard_map/while/body/eval_jaxpr/dot_general | solution.py:96
  338.9 14.2 %all-to-all-done = bf16[32,16,512]{2,0,1:T(8,128)(2,1)S(1)} async-done(((bf16[32,16,512]{2,0,1:T(8,128)(2,1)}), bf16[32,16,512]{2,0,1:T(8,128)(2,1)S(1)}, u32[]{:S(2)}, u32[]{:S(2)}) %all-to-all-start) | async-done | bytes 524320 | tf_op jit(solution)/shard_map/while/body/eval_jaxpr/all_to_all | solution.py:99
  359.1 5.9 %convolution_convert_fusion.2 = bf16[32,8192]{1,0:T(8,128)(2,1)S(1)} fusion(bf16[8192,512]{1,0:T(8,128)(2,1)} %get-tuple-element.748, f32[4,32,512]{2,1,0:T(8,128)S(1)} %get-tuple-element.747, s32[]{:T(128)S(6)} %min.21, bf16[32,512]{1,0:T(8,128)(2,1)S(1)} %get-tuple-element.725, f32[512]{0:T(512)S(1)} %get-tuple-element.746, f32[32]{0:T(128)S(1)} %fusion.37, ...), kind=kOutput, calls=%fused_computation.12.clone.1 | convolution fusion | flops 268910592 | bytes 9013765 | tf_op jit(solution)/shard_map/while/body/eval_jaxpr/dot_general | solution.py:96
  370.1 14.2 %all-to-all-done = bf16[32,16,512]{2,0,1:T(8,128)(2,1)S(1)} async-done(((bf16[32,16,512]{2,0,1:T(8,128)(2,1)}), bf16[32,16,512]{2,0,1:T(8,128)(2,1)S(1)}, u32[]{:S(2)}, u32[]{:S(2)}) %all-to-all-start) | async-done | bytes 524320 | tf_op jit(solution)/shard_map/while/body/eval_jaxpr/all_to_all | solution.py:99
  390.4 5.9 %convolution_convert_fusion.2 = bf16[32,8192]{1,0:T(8,128)(2,1)S(1)} fusion(bf16[8192,512]{1,0:T(8,128)(2,1)} %get-tuple-element.748, f32[4,32,512]{2,1,0:T(8,128)S(1)} %get-tuple-element.747, s32[]{:T(128)S(6)} %min.21, bf16[32,512]{1,0:T(8,128)(2,1)S(1)} %get-tuple-element.725, f32[512]{0:T(512)S(1)} %get-tuple-element.746, f32[32]{0:T(128)S(1)} %fusion.37, ...), kind=kOutput, calls=%fused_computation.12.clone.1 | convolution fusion | flops 268910592 | bytes 9013765 | tf_op jit(solution)/shard_map/while/body/eval_jaxpr/dot_general | solution.py:96
  401.3 14.2 %all-to-all-done = bf16[32,16,512]{2,0,1:T(8,128)(2,1)S(1)} async-done(((bf16[32,16,512]{2,0,1:T(8,128)(2,1)}), bf16[32,16,512]{2,0,1:T(8,128)(2,1)S(1)}, u32[]{:S(2)}, u32[]{:S(2)}) %all-to-all-start) | async-done | bytes 524320 | tf_op jit(solution)/shard_map/while/body/eval_jaxpr/all_to_all | solution.py:99
  421.6 5.9 %convolution_convert_fusion.2 = bf16[32,8192]{1,0:T(8,128)(2,1)S(1)} fusion(bf16[8192,512]{1,0:T(8,128)(2,1)} %get-tuple-element.748, f32[4,32,512]{2,1,0:T(8,128)S(1)} %get-tuple-element.747, s32[]{:T(128)S(6)} %min.21, bf16[32,512]{1,0:T(8,128)(2,1)S(1)} %get-tuple-element.725, f32[512]{0:T(512)S(1)} %get-tuple-element.746, f32[32]{0:T(128)S(1)} %fusion.37, ...), kind=kOutput, calls=%fused_computation.12.clone.1 | convolution fusion | flops 268910592 | bytes 9013765 | tf_op jit(solution)/shard_map/while/body/eval_jaxpr/dot_general | solution.py:96
  432.6 14.2 %all-to-all-done = bf16[32,16,512]{2,0,1:T(8,128)(2,1)S(1)} async-done(((bf16[32,16,512]{2,0,1:T(8,128)(2,1)}), bf16[32,16,512]{2,0,1:T(8,128)(2,1)S(1)}, u32[]{:S(2)}, u32[]{:S(2)}) %all-to-all-start) | async-done | bytes 524320 | tf_op jit(solution)/shard_map/while/body/eval_jaxpr/all_to_all | solution.py:99
  452.8 8.5 %fusion.13 = (f32[]{:T(128)}, bf16[1,8192,512]{2,1,0:T(8,128)(2,1)}) fusion(bf16[1,8192,512]{2,1,0:T(8,128)(2,1)} %bitcast.111, f32[]{:T(128)} %sqrt.3, bf16[4,32,8192]{2,1,0:T(8,128)(2,1)S(1)} %get-tuple-element.460, bf16[4,32,512]{2,1,0:T(8,128)(2,1)S(1)} %get-tuple-element.463), kind=kOutput, calls=%fused_computation.40 | convolution fusion | flops 1094713344 | bytes 19005448 | tf_op jit(solution)/shard_map/dot_general | solution.py:115
  461.3 31.7 %psum.31 = f32[]{:T(128)} all-reduce(f32[]{:T(128)} %get-tuple-element.513), channel_id=1, replica_groups=mesh['section'=2,'mp'=16] {'mp'}, use_global_device_ids=true, to_apply=%region_12.13 | all-reduce | flops 1 | bytes 8 | tf_op jit(solution)/shard_map/psum | solution.py:119
  (114 shorter events, 118.2 us)
Async XLA Ops:
  70.6 36.8 %copy-start = (f32[512]{0:T(512)S(1)}, f32[512]{0:T(512)}, u32[]{:S(2)}) copy-start(f32[512]{0:T(512)} %param.13) | copy-start | bytes 6148
  132.5 5.3 %collective-permute-start = (bf16[32,512]{1,0:T(8,128)(2,1)}, bf16[32,512]{1,0:T(8,128)(2,1)}, u32[]{:S(2)}, u32[]{:S(2)}) collective-permute-start(bf16[32,512]{1,0:T(8,128)(2,1)} %get-tuple-element.647), channel_id=1, source_target_pairs={{0,16},{1,17},{2,18},{3,19},{4,20},{5,21},{6,22},{7,23},{8,24},{9,... | collective-permute-start | bytes 98312 | tf_op jit(solution)/shard_map/while/body/eval_jaxpr/ppermute | solution.py:13
  164.7 6.1 %collective-permute-start = (bf16[32,512]{1,0:T(8,128)(2,1)}, bf16[32,512]{1,0:T(8,128)(2,1)}, u32[]{:S(2)}, u32[]{:S(2)}) collective-permute-start(bf16[32,512]{1,0:T(8,128)(2,1)} %get-tuple-element.647), channel_id=1, source_target_pairs={{0,16},{1,17},{2,18},{3,19},{4,20},{5,21},{6,22},{7,23},{8,24},{9,... | collective-permute-start | bytes 98312 | tf_op jit(solution)/shard_map/while/body/eval_jaxpr/ppermute | solution.py:13
  195.9 6.1 %collective-permute-start = (bf16[32,512]{1,0:T(8,128)(2,1)}, bf16[32,512]{1,0:T(8,128)(2,1)}, u32[]{:S(2)}, u32[]{:S(2)}) collective-permute-start(bf16[32,512]{1,0:T(8,128)(2,1)} %get-tuple-element.647), channel_id=1, source_target_pairs={{0,16},{1,17},{2,18},{3,19},{4,20},{5,21},{6,22},{7,23},{8,24},{9,... | collective-permute-start | bytes 98312 | tf_op jit(solution)/shard_map/while/body/eval_jaxpr/ppermute | solution.py:13
  228.9 6.1 %collective-permute-start = (bf16[32,512]{1,0:T(8,128)(2,1)}, bf16[32,512]{1,0:T(8,128)(2,1)}, u32[]{:S(2)}, u32[]{:S(2)}) collective-permute-start(bf16[32,512]{1,0:T(8,128)(2,1)} %get-tuple-element.647), channel_id=1, source_target_pairs={{0,16},{1,17},{2,18},{3,19},{4,20},{5,21},{6,22},{7,23},{8,24},{9,... | collective-permute-start | bytes 98312 | tf_op jit(solution)/shard_map/while/body/eval_jaxpr/ppermute | solution.py:13
  260.1 6.1 %collective-permute-start = (bf16[32,512]{1,0:T(8,128)(2,1)}, bf16[32,512]{1,0:T(8,128)(2,1)}, u32[]{:S(2)}, u32[]{:S(2)}) collective-permute-start(bf16[32,512]{1,0:T(8,128)(2,1)} %get-tuple-element.647), channel_id=1, source_target_pairs={{0,16},{1,17},{2,18},{3,19},{4,20},{5,21},{6,22},{7,23},{8,24},{9,... | collective-permute-start | bytes 98312 | tf_op jit(solution)/shard_map/while/body/eval_jaxpr/ppermute | solution.py:13
  304.2 17.8 %all-to-all-start = ((bf16[32,16,512]{2,0,1:T(8,128)(2,1)}), bf16[32,16,512]{2,0,1:T(8,128)(2,1)S(1)}, u32[]{:S(2)}, u32[]{:S(2)}) async-start(bf16[32,16,512]{2,0,1:T(8,128)(2,1)} %bitcast.109), calls=%async_computation | async-start | bytes 1048576 | tf_op jit(solution)/shard_map/while/body/eval_jaxpr/all_to_all | solution.py:99
  322.2 5.8 %collective-permute-start.1 = (bf16[32,512]{1,0:T(8,128)(2,1)S(1)}, bf16[32,512]{1,0:T(8,128)(2,1)S(1)}, u32[]{:S(2)}, u32[]{:S(2)}) collective-permute-start(bf16[32,512]{1,0:T(8,128)(2,1)S(1)} %fusion.38), channel_id=1, source_target_pairs={{16,0},{17,1},{18,2},{19,3},{20,4},{21,5},{22,6},{23,7},{24,8},{25... | collective-permute-start | bytes 98312 | tf_op jit(solution)/shard_map/while/body/eval_jaxpr/ppermute | solution.py:13
  334.8 18.4 %all-to-all-start = ((bf16[32,16,512]{2,0,1:T(8,128)(2,1)}), bf16[32,16,512]{2,0,1:T(8,128)(2,1)S(1)}, u32[]{:S(2)}, u32[]{:S(2)}) async-start(bf16[32,16,512]{2,0,1:T(8,128)(2,1)} %bitcast.109), calls=%async_computation | async-start | bytes 1048576 | tf_op jit(solution)/shard_map/while/body/eval_jaxpr/all_to_all | solution.py:99
  353.3 5.8 %collective-permute-start.1 = (bf16[32,512]{1,0:T(8,128)(2,1)S(1)}, bf16[32,512]{1,0:T(8,128)(2,1)S(1)}, u32[]{:S(2)}, u32[]{:S(2)}) collective-permute-start(bf16[32,512]{1,0:T(8,128)(2,1)S(1)} %fusion.38), channel_id=1, source_target_pairs={{16,0},{17,1},{18,2},{19,3},{20,4},{21,5},{22,6},{23,7},{24,8},{25... | collective-permute-start | bytes 98312 | tf_op jit(solution)/shard_map/while/body/eval_jaxpr/ppermute | solution.py:13
  365.9 18.4 %all-to-all-start = ((bf16[32,16,512]{2,0,1:T(8,128)(2,1)}), bf16[32,16,512]{2,0,1:T(8,128)(2,1)S(1)}, u32[]{:S(2)}, u32[]{:S(2)}) async-start(bf16[32,16,512]{2,0,1:T(8,128)(2,1)} %bitcast.109), calls=%async_computation | async-start | bytes 1048576 | tf_op jit(solution)/shard_map/while/body/eval_jaxpr/all_to_all | solution.py:99
  384.5 5.8 %collective-permute-start.1 = (bf16[32,512]{1,0:T(8,128)(2,1)S(1)}, bf16[32,512]{1,0:T(8,128)(2,1)S(1)}, u32[]{:S(2)}, u32[]{:S(2)}) collective-permute-start(bf16[32,512]{1,0:T(8,128)(2,1)S(1)} %fusion.38), channel_id=1, source_target_pairs={{16,0},{17,1},{18,2},{19,3},{20,4},{21,5},{22,6},{23,7},{24,8},{25... | collective-permute-start | bytes 98312 | tf_op jit(solution)/shard_map/while/body/eval_jaxpr/ppermute | solution.py:13
  397.2 18.4 %all-to-all-start = ((bf16[32,16,512]{2,0,1:T(8,128)(2,1)}), bf16[32,16,512]{2,0,1:T(8,128)(2,1)S(1)}, u32[]{:S(2)}, u32[]{:S(2)}) async-start(bf16[32,16,512]{2,0,1:T(8,128)(2,1)} %bitcast.109), calls=%async_computation | async-start | bytes 1048576 | tf_op jit(solution)/shard_map/while/body/eval_jaxpr/all_to_all | solution.py:99
  415.8 5.8 %collective-permute-start.1 = (bf16[32,512]{1,0:T(8,128)(2,1)S(1)}, bf16[32,512]{1,0:T(8,128)(2,1)S(1)}, u32[]{:S(2)}, u32[]{:S(2)}) collective-permute-start(bf16[32,512]{1,0:T(8,128)(2,1)S(1)} %fusion.38), channel_id=1, source_target_pairs={{16,0},{17,1},{18,2},{19,3},{20,4},{21,5},{22,6},{23,7},{24,8},{25... | collective-permute-start | bytes 98312 | tf_op jit(solution)/shard_map/while/body/eval_jaxpr/ppermute | solution.py:13
  428.4 18.4 %all-to-all-start = ((bf16[32,16,512]{2,0,1:T(8,128)(2,1)}), bf16[32,16,512]{2,0,1:T(8,128)(2,1)S(1)}, u32[]{:S(2)}, u32[]{:S(2)}) async-start(bf16[32,16,512]{2,0,1:T(8,128)(2,1)} %bitcast.109), calls=%async_computation | async-start | bytes 1048576 | tf_op jit(solution)/shard_map/while/body/eval_jaxpr/all_to_all | solution.py:99
  447.0 5.8 %collective-permute-start.1 = (bf16[32,512]{1,0:T(8,128)(2,1)S(1)}, bf16[32,512]{1,0:T(8,128)(2,1)S(1)}, u32[]{:S(2)}, u32[]{:S(2)}) collective-permute-start(bf16[32,512]{1,0:T(8,128)(2,1)S(1)} %fusion.38), channel_id=1, source_target_pairs={{16,0},{17,1},{18,2},{19,3},{20,4},{21,5},{22,6},{23,7},{24,8},{25... | collective-permute-start | bytes 98312 | tf_op jit(solution)/shard_map/while/body/eval_jaxpr/ppermute | solution.py:13
where the time goes:
time: 497 us; the launch traced here: 495 us
  blocking collectives  252 us (51%)
  waiting for transfers between devices  98.3 us (20%)
  matrix products  76.6 us (15%)
  starting transfers between devices  49.8 us (10%)
  other arithmetic  8.44 us (2%)
  local copies, waits for them, and re-layouts  5.69 us (1%)
    all_gather x5, blocking collectives, forward_tick(): shard_piece = lax.all_gather(layer_in, 'mp', axis=1, tiled=True)  97 us
    all_to_all x5, waiting for transfers between devices, backward_tick(): lax.all_to_all(partial_term.astype(jnp.bfloat16), 'mp', split_axis=1, con...  71.2 us
    psum x1, blocking collectives, power_step(): lax.psum(jnp.dot(weight, vector_bf, preferred_element_type=jnp.float32),...  63 us
    psum x1, blocking collectives, on_device(): lax.psum(jnp.sum(outer_sum * weight.astype(jnp.float32)), 'mp')  31.7 us
    psum x1, blocking collectives, on_device(): logits_all = lax.psum(partial_logits, 'mp')  30.4 us
    psum x1, blocking collectives, power_step(): norm_total = lax.psum(jnp.sum(right_part * right_part), 'mp')  30.1 us
    ppermute x10, starting transfers between devices, shifted(): return lax.ppermute(block, axis, route)  29.6 us
    dot_general x5, matrix products, backward_tick(): lax.dot_general(grad_pre, weight, (((1,), (1,)), ((), ())), preferred_ele...  29.6 us
  transfers between devices with their start and end apart: 15, of which 15 were waited for; matrix products, arithmetic and copies ran while one was open for 0% of the time, Pallas kernels for 0%

commit v1 on v0

--- a/solution.py
+++ b/solution.py
@@ -27,7 +27,9 @@
 
 def power_step(weight, vector_u):
     vector_bf = vector_u.astype(jnp.bfloat16)
-    left_sum = lax.psum(jnp.dot(weight, vector_bf, preferred_element_type=jnp.float32), "mp")
+    left_sum = jnp.sum(
+        lax.all_gather(jnp.dot(weight, vector_bf, preferred_element_type=jnp.float32), "mp"), axis=0
+    )
     vector_v = (left_sum * lax.rsqrt(jnp.sum(left_sum * left_sum) + tiny_eps)).astype(jnp.bfloat16)
     right_part = jnp.dot(vector_v, weight, preferred_element_type=jnp.float32)
     norm_total = lax.psum(jnp.sum(right_part * right_part), "mp")

time: 497 us -> 459 us (0.924)
  blocking collectives: 252 us -> 214 us
    psum x1 -> x0, blocking collectives: 63 us -> none  [power_step(): lax.psum(jnp.dot(weight, vector_bf, preferred_element_type=jnp.float32),...]
    all_gather x0 -> x1, blocking collectives: none -> 24.6 us  [power_step(): lax.all_gather(jnp.dot(weight, vector_bf, preferred_element_type=jnp.floa...]
where the time goes in v1:
time: 459 us; the launch traced here: 458 us
  blocking collectives  214 us (47%)
  waiting for transfers between devices  98.3 us (21%)
  matrix products  76.6 us (17%)
  starting transfers between devices  49.8 us (11%)
  other arithmetic  8.52 us (2%)
  local copies, waits for them, and re-layouts  5.79 us (1%)
    all_gather x5, blocking collectives, forward_tick(): shard_piece = lax.all_gather(layer_in, 'mp', axis=1, tiled=True)  97 us
    all_to_all x5, waiting for transfers between devices, backward_tick(): lax.all_to_all(partial_term.astype(jnp.bfloat16), 'mp', split_axis=1, con...  71.2 us
    psum x1, blocking collectives, on_device(): lax.psum(jnp.sum(outer_sum * weight.astype(jnp.float32)), 'mp')  31.7 us
    psum x1, blocking collectives, power_step(): norm_total = lax.psum(jnp.sum(right_part * right_part), 'mp')  30.4 us
    psum x1, blocking collectives, on_device(): logits_all = lax.psum(partial_logits, 'mp')  30.3 us
    ppermute x10, starting transfers between devices, shifted(): return lax.ppermute(block, axis, route)  29.7 us
    dot_general x5, matrix products, backward_tick(): lax.dot_general(grad_pre, weight, (((1,), (1,)), ((), ())), preferred_ele...  29.6 us
    dot_general x5, matrix products, forward_tick(): jnp.dot(shard_piece, weight, preferred_element_type=jnp.float32)  28.3 us
  transfers between devices with their start and end apart: 15, of which 15 were waited for; matrix products, arithmetic and copies ran while one was open for 0% of the time, Pallas kernels for 0%

profile of v1, /device:TPU:0, one launch (start us, length us, event | category | flops | bytes accessed | tf_op | source)
XLA Modules:
  0.0 457.5 jit_solution(6151154486589037833)
XLA Ops:
  6.3 24.6 %all-gather = f32[131072]{0:T(1024)S(1)} all-gather(f32[8192]{0:T(1024)S(1)} %bitcast.113), channel_id=2, replica_groups=mesh['section'=2,'mp'=16] {'mp'}, dimensions={0}, use_global_device_ids=true | all-gather | bytes 557056 | tf_op jit(solution)/shard_map/all_gather | solution.py:31
  37.6 30.4 %psum.21 = f32[]{:T(128)} all-reduce(f32[]{:T(128)} %multiply_reduce_fusion.2), channel_id=1, replica_groups=mesh['section'=2,'mp'=16] {'mp'}, use_global_device_ids=true, to_apply=%region_3.0 | all-reduce | flops 1 | bytes 8 | tf_op jit(solution)/shard_map/psum | solution.py:35
  69.6 158.9 %while.37 = (s32[]{:T(128)}, bf16[32,512]{1,0:T(8,128)(2,1)}, bf16[4,32,8192]{2,1,0:T(8,128)(2,1)S(1)}, f32[4,32,512]{2,1,0:T(8,128)S(1)}, f32[4,32]{1,0:T(4,128...) while((s32[]{:T(128)}, bf16[32,512]{1,0:T(8,128)(2,1)}, ...), condition=%wide.region_6.7_spmd, body=%wide.region_4.6_spmd.sunk | while | flops 268910592 | bytes 12782621 | solution.py:81
  70.4 18.8 %all_gather.17 = bf16[32,8192]{1,0:T(8,128)(2,1)S(1)} all-gather(bf16[32,512]{1,0:T(8,128)(2,1)S(1)} %bitcast_select_fusion.5), channel_id=1, replica_groups=mesh['section'=2,'mp'=16] {'mp'}, dimensions={1}, use_global_device_ids=true | all-gather | bytes 557056 | tf_op jit(solution)/shard_map/while/body/eval_jaxpr/all_gather | solution.py:58
  89.1 5.7 %multiply_reduce_fusion.4 = (f32[32]{0:T(128)S(1)}, bf16[32,512]{1,0:T(8,128)(2,1)}, f32[32,512]{1,0:T(8,128)S(1)}) fusion(f32[512]{0:T(512)S(1)} %get-tuple-element.704, bf16[32,512]{1,0:T(8,128)(2,1)S(1)} %bitcast_select_fusion.5, f32[]{:T(128)} %get-tuple-element.702, bf16[32,8192]{1,0:T(8,128)(2,1)S(1)} %all_gather.17, ...), kind=kOutput, calls=%fused_computation.5.clone.1 | convolution fusion | flops 268615648 | bytes 9046148 | tf_op jit(solution)/shard_map/while/body/eval_jaxpr/dot_general | solution.py:59
  100.9 20.4 %all_gather.17 = bf16[32,8192]{1,0:T(8,128)(2,1)S(1)} all-gather(bf16[32,512]{1,0:T(8,128)(2,1)S(1)} %bitcast_select_fusion.5), channel_id=1, replica_groups=mesh['section'=2,'mp'=16] {'mp'}, dimensions={1}, use_global_device_ids=true | all-gather | bytes 557056 | tf_op jit(solution)/shard_map/while/body/eval_jaxpr/all_gather | solution.py:58
  121.3 5.7 %multiply_reduce_fusion.4 = (f32[32]{0:T(128)S(1)}, bf16[32,512]{1,0:T(8,128)(2,1)}, f32[32,512]{1,0:T(8,128)S(1)}) fusion(f32[512]{0:T(512)S(1)} %get-tuple-element.704, bf16[32,512]{1,0:T(8,128)(2,1)S(1)} %bitcast_select_fusion.5, f32[]{:T(128)} %get-tuple-element.702, bf16[32,8192]{1,0:T(8,128)(2,1)S(1)} %all_gather.17, ...), kind=kOutput, calls=%fused_computation.5.clone.1 | convolution fusion | flops 268615648 | bytes 9046148 | tf_op jit(solution)/shard_map/while/body/eval_jaxpr/dot_general | solution.py:59
  133.7 18.8 %all_gather.17 = bf16[32,8192]{1,0:T(8,128)(2,1)S(1)} all-gather(bf16[32,512]{1,0:T(8,128)(2,1)S(1)} %bitcast_select_fusion.5), channel_id=1, replica_groups=mesh['section'=2,'mp'=16] {'mp'}, dimensions={1}, use_global_device_ids=true | all-gather | bytes 557056 | tf_op jit(solution)/shard_map/while/body/eval_jaxpr/all_gather | solution.py:58
  165.1 20.4 %all_gather.17 = bf16[32,8192]{1,0:T(8,128)(2,1)S(1)} all-gather(bf16[32,512]{1,0:T(8,128)(2,1)S(1)} %bitcast_select_fusion.5), channel_id=1, replica_groups=mesh['section'=2,'mp'=16] {'mp'}, dimensions={1}, use_global_device_ids=true | all-gather | bytes 557056 | tf_op jit(solution)/shard_map/while/body/eval_jaxpr/all_gather | solution.py:58
  197.9 18.8 %all_gather.17 = bf16[32,8192]{1,0:T(8,128)(2,1)S(1)} all-gather(bf16[32,512]{1,0:T(8,128)(2,1)S(1)} %bitcast_select_fusion.5), channel_id=1, replica_groups=mesh['section'=2,'mp'=16] {'mp'}, dimensions={1}, use_global_device_ids=true | all-gather | bytes 557056 | tf_op jit(solution)/shard_map/while/body/eval_jaxpr/all_gather | solution.py:58
  228.5 30.3 %psum.22 = f32[4,32]{1,0:T(4,128)S(1)} all-reduce(f32[4,32]{1,0:T(4,128)S(1)} %get-tuple-element.461), channel_id=1, replica_groups=mesh['section'=2,'mp'=16] {'mp'}, use_global_device_ids=true, to_apply=%region_7.8 | all-reduce | flops 128 | bytes 1024 | tf_op jit(solution)/shard_map/psum | solution.py:84
  259.5 155.4 %while.38 = (s32[]{:T(128)}, bf16[32,512]{1,0:T(8,128)(2,1)S(1)}, bf16[4,32,512]{2,1,0:T(8,128)(2,1)S(1)}, pred[]{:T(512)}, s32[]{:T(128)}, /*index=5*/f32[4,32]...) while((s32[]{:T(128)}, bf16[32,512]{1,0:T(8,128)(2,1)S(1)}, ...), condition=%wide.region_10.11_spmd, body=%wide.region_8.10_spmd.sunk | while | flops 269762784 | bytes 12787494 | solution.py:114
  259.6 5.9 %convolution_convert_fusion.2 = bf16[32,8192]{1,0:T(8,128)(2,1)S(1)} fusion(bf16[8192,512]{1,0:T(8,128)(2,1)} %get-tuple-element.748, f32[4,32,512]{2,1,0:T(8,128)S(1)} %get-tuple-element.747, s32[]{:T(128)S(6)} %min.21, bf16[32,512]{1,0:T(8,128)(2,1)S(1)} %get-tuple-element.725, f32[512]{0:T(512)S(1)} %get-tuple-element.746, f32[32]{0:T(128)S(1)} %fusion.37, ...), kind=kOutput, calls=%fused_computation.12.clone.1 | convolution fusion | flops 268910592 | bytes 9013765 | tf_op jit(solution)/shard_map/while/body/eval_jaxpr/dot_general | solution.py:98
  270.0 14.2 %all-to-all-done = bf16[32,16,512]{2,0,1:T(8,128)(2,1)S(1)} async-done(((bf16[32,16,512]{2,0,1:T(8,128)(2,1)}), bf16[32,16,512]{2,0,1:T(8,128)(2,1)S(1)}, u32[]{:S(2)}, u32[]{:S(2)}) %all-to-all-start) | async-done | bytes 524320 | tf_op jit(solution)/shard_map/while/body/eval_jaxpr/all_to_all | solution.py:101
  290.1 5.9 %convolution_convert_fusion.2 = bf16[32,8192]{1,0:T(8,128)(2,1)S(1)} fusion(bf16[8192,512]{1,0:T(8,128)(2,1)} %get-tuple-element.748, f32[4,32,512]{2,1,0:T(8,128)S(1)} %get-tuple-element.747, s32[]{:T(128)S(6)} %min.21, bf16[32,512]{1,0:T(8,128)(2,1)S(1)} %get-tuple-element.725, f32[512]{0:T(512)S(1)} %get-tuple-element.746, f32[32]{0:T(128)S(1)} %fusion.37, ...), kind=kOutput, calls=%fused_computation.12.clone.1 | convolution fusion | flops 268910592 | bytes 9013765 | tf_op jit(solution)/shard_map/while/body/eval_jaxpr/dot_general | solution.py:98
  301.1 14.2 %all-to-all-done = bf16[32,16,512]{2,0,1:T(8,128)(2,1)S(1)} async-done(((bf16[32,16,512]{2,0,1:T(8,128)(2,1)}), bf16[32,16,512]{2,0,1:T(8,128)(2,1)S(1)}, u32[]{:S(2)}, u32[]{:S(2)}) %all-to-all-start) | async-done | bytes 524320 | tf_op jit(solution)/shard_map/while/body/eval_jaxpr/all_to_all | solution.py:101
  321.3 5.9 %convolution_convert_fusion.2 = bf16[32,8192]{1,0:T(8,128)(2,1)S(1)} fusion(bf16[8192,512]{1,0:T(8,128)(2,1)} %get-tuple-element.748, f32[4,32,512]{2,1,0:T(8,128)S(1)} %get-tuple-element.747, s32[]{:T(128)S(6)} %min.21, bf16[32,512]{1,0:T(8,128)(2,1)S(1)} %get-tuple-element.725, f32[512]{0:T(512)S(1)} %get-tuple-element.746, f32[32]{0:T(128)S(1)} %fusion.37, ...), kind=kOutput, calls=%fused_computation.12.clone.1 | convolution fusion | flops 268910592 | bytes 9013765 | tf_op jit(solution)/shard_map/while/body/eval_jaxpr/dot_general | solution.py:98
  332.3 14.2 %all-to-all-done = bf16[32,16,512]{2,0,1:T(8,128)(2,1)S(1)} async-done(((bf16[32,16,512]{2,0,1:T(8,128)(2,1)}), bf16[32,16,512]{2,0,1:T(8,128)(2,1)S(1)}, u32[]{:S(2)}, u32[]{:S(2)}) %all-to-all-start) | async-done | bytes 524320 | tf_op jit(solution)/shard_map/while/body/eval_jaxpr/all_to_all | solution.py:101
  352.5 5.9 %convolution_convert_fusion.2 = bf16[32,8192]{1,0:T(8,128)(2,1)S(1)} fusion(bf16[8192,512]{1,0:T(8,128)(2,1)} %get-tuple-element.748, f32[4,32,512]{2,1,0:T(8,128)S(1)} %get-tuple-element.747, s32[]{:T(128)S(6)} %min.21, bf16[32,512]{1,0:T(8,128)(2,1)S(1)} %get-tuple-element.725, f32[512]{0:T(512)S(1)} %get-tuple-element.746, f32[32]{0:T(128)S(1)} %fusion.37, ...), kind=kOutput, calls=%fused_computation.12.clone.1 | convolution fusion | flops 268910592 | bytes 9013765 | tf_op jit(solution)/shard_map/while/body/eval_jaxpr/dot_general | solution.py:98
  363.5 14.2 %all-to-all-done = bf16[32,16,512]{2,0,1:T(8,128)(2,1)S(1)} async-done(((bf16[32,16,512]{2,0,1:T(8,128)(2,1)}), bf16[32,16,512]{2,0,1:T(8,128)(2,1)S(1)}, u32[]{:S(2)}, u32[]{:S(2)}) %all-to-all-start) | async-done | bytes 524320 | tf_op jit(solution)/shard_map/while/body/eval_jaxpr/all_to_all | solution.py:101
  383.7 5.9 %convolution_convert_fusion.2 = bf16[32,8192]{1,0:T(8,128)(2,1)S(1)} fusion(bf16[8192,512]{1,0:T(8,128)(2,1)} %get-tuple-element.748, f32[4,32,512]{2,1,0:T(8,128)S(1)} %get-tuple-element.747, s32[]{:T(128)S(6)} %min.21, bf16[32,512]{1,0:T(8,128)(2,1)S(1)} %get-tuple-element.725, f32[512]{0:T(512)S(1)} %get-tuple-element.746, f32[32]{0:T(128)S(1)} %fusion.37, ...), kind=kOutput, calls=%fused_computation.12.clone.1 | convolution fusion | flops 268910592 | bytes 9013765 | tf_op jit(solution)/shard_map/while/body/eval_jaxpr/dot_general | solution.py:98
  394.7 14.2 %all-to-all-done = bf16[32,16,512]{2,0,1:T(8,128)(2,1)S(1)} async-done(((bf16[32,16,512]{2,0,1:T(8,128)(2,1)}), bf16[32,16,512]{2,0,1:T(8,128)(2,1)S(1)}, u32[]{:S(2)}, u32[]{:S(2)}) %all-to-all-start) | async-done | bytes 524320 | tf_op jit(solution)/shard_map/while/body/eval_jaxpr/all_to_all | solution.py:101
  414.9 8.5 %fusion.13 = (f32[]{:T(128)}, bf16[1,8192,512]{2,1,0:T(8,128)(2,1)}) fusion(bf16[1,8192,512]{2,1,0:T(8,128)(2,1)} %bitcast.111, f32[]{:T(128)} %sqrt.3, bf16[4,32,8192]{2,1,0:T(8,128)(2,1)S(1)} %get-tuple-element.460, bf16[4,32,512]{2,1,0:T(8,128)(2,1)S(1)} %get-tuple-element.463), kind=kOutput, calls=%fused_computation.40 | convolution fusion | flops 1094713344 | bytes 19005448 | tf_op jit(solution)/shard_map/dot_general | solution.py:117
  423.4 31.7 %psum.23 = f32[]{:T(128)} all-reduce(f32[]{:T(128)} %get-tuple-element.513), channel_id=1, replica_groups=mesh['section'=2,'mp'=16] {'mp'}, use_global_device_ids=true, to_apply=%region_12.13 | all-reduce | flops 1 | bytes 8 | tf_op jit(solution)/shard_map/psum | solution.py:121
  (116 shorter events, 118.4 us)
Async XLA Ops:
  32.4 37.2 %copy-start = (f32[512]{0:T(512)S(1)}, f32[512]{0:T(512)}, u32[]{:S(2)}) copy-start(f32[512]{0:T(512)} %param.13) | copy-start | bytes 6148
  94.8 5.3 %collective-permute-start = (bf16[32,512]{1,0:T(8,128)(2,1)}, bf16[32,512]{1,0:T(8,128)(2,1)}, u32[]{:S(2)}, u32[]{:S(2)}) collective-permute-start(bf16[32,512]{1,0:T(8,128)(2,1)} %get-tuple-element.647), channel_id=1, source_target_pairs={{0,16},{1,17},{2,18},{3,19},{4,20},{5,21},{6,22},{7,23},{8,24},{9,... | collective-permute-start | bytes 98312 | tf_op jit(solution)/shard_map/while/body/eval_jaxpr/ppermute | solution.py:13
  126.9 6.0 %collective-permute-start = (bf16[32,512]{1,0:T(8,128)(2,1)}, bf16[32,512]{1,0:T(8,128)(2,1)}, u32[]{:S(2)}, u32[]{:S(2)}) collective-permute-start(bf16[32,512]{1,0:T(8,128)(2,1)} %get-tuple-element.647), channel_id=1, source_target_pairs={{0,16},{1,17},{2,18},{3,19},{4,20},{5,21},{6,22},{7,23},{8,24},{9,... | collective-permute-start | bytes 98312 | tf_op jit(solution)/shard_map/while/body/eval_jaxpr/ppermute | solution.py:13
  158.2 6.1 %collective-permute-start = (bf16[32,512]{1,0:T(8,128)(2,1)}, bf16[32,512]{1,0:T(8,128)(2,1)}, u32[]{:S(2)}, u32[]{:S(2)}) collective-permute-start(bf16[32,512]{1,0:T(8,128)(2,1)} %get-tuple-element.647), channel_id=1, source_target_pairs={{0,16},{1,17},{2,18},{3,19},{4,20},{5,21},{6,22},{7,23},{8,24},{9,... | collective-permute-start | bytes 98312 | tf_op jit(solution)/shard_map/while/body/eval_jaxpr/ppermute | solution.py:13
  191.1 6.0 %collective-permute-start = (bf16[32,512]{1,0:T(8,128)(2,1)}, bf16[32,512]{1,0:T(8,128)(2,1)}, u32[]{:S(2)}, u32[]{:S(2)}) collective-permute-start(bf16[32,512]{1,0:T(8,128)(2,1)} %get-tuple-element.647), channel_id=1, source_target_pairs={{0,16},{1,17},{2,18},{3,19},{4,20},{5,21},{6,22},{7,23},{8,24},{9,... | collective-permute-start | bytes 98312 | tf_op jit(solution)/shard_map/while/body/eval_jaxpr/ppermute | solution.py:13
  222.3 6.1 %collective-permute-start = (bf16[32,512]{1,0:T(8,128)(2,1)}, bf16[32,512]{1,0:T(8,128)(2,1)}, u32[]{:S(2)}, u32[]{:S(2)}) collective-permute-start(bf16[32,512]{1,0:T(8,128)(2,1)} %get-tuple-element.647), channel_id=1, source_target_pairs={{0,16},{1,17},{2,18},{3,19},{4,20},{5,21},{6,22},{7,23},{8,24},{9,... | collective-permute-start | bytes 98312 | tf_op jit(solution)/shard_map/while/body/eval_jaxpr/ppermute | solution.py:13
  266.3 17.8 %all-to-all-start = ((bf16[32,16,512]{2,0,1:T(8,128)(2,1)}), bf16[32,16,512]{2,0,1:T(8,128)(2,1)S(1)}, u32[]{:S(2)}, u32[]{:S(2)}) async-start(bf16[32,16,512]{2,0,1:T(8,128)(2,1)} %bitcast.109), calls=%async_computation | async-start | bytes 1048576 | tf_op jit(solution)/shard_map/while/body/eval_jaxpr/all_to_all | solution.py:101
  284.3 5.8 %collective-permute-start.1 = (bf16[32,512]{1,0:T(8,128)(2,1)S(1)}, bf16[32,512]{1,0:T(8,128)(2,1)S(1)}, u32[]{:S(2)}, u32[]{:S(2)}) collective-permute-start(bf16[32,512]{1,0:T(8,128)(2,1)S(1)} %fusion.38), channel_id=1, source_target_pairs={{16,0},{17,1},{18,2},{19,3},{20,4},{21,5},{22,6},{23,7},{24,8},{25... | collective-permute-start | bytes 98312 | tf_op jit(solution)/shard_map/while/body/eval_jaxpr/ppermute | solution.py:13
  296.9 18.4 %all-to-all-start = ((bf16[32,16,512]{2,0,1:T(8,128)(2,1)}), bf16[32,16,512]{2,0,1:T(8,128)(2,1)S(1)}, u32[]{:S(2)}, u32[]{:S(2)}) async-start(bf16[32,16,512]{2,0,1:T(8,128)(2,1)} %bitcast.109), calls=%async_computation | async-start | bytes 1048576 | tf_op jit(solution)/shard_map/while/body/eval_jaxpr/all_to_all | solution.py:101
  315.5 5.8 %collective-permute-start.1 = (bf16[32,512]{1,0:T(8,128)(2,1)S(1)}, bf16[32,512]{1,0:T(8,128)(2,1)S(1)}, u32[]{:S(2)}, u32[]{:S(2)}) collective-permute-start(bf16[32,512]{1,0:T(8,128)(2,1)S(1)} %fusion.38), channel_id=1, source_target_pairs={{16,0},{17,1},{18,2},{19,3},{20,4},{21,5},{22,6},{23,7},{24,8},{25... | collective-permute-start | bytes 98312 | tf_op jit(solution)/shard_map/while/body/eval_jaxpr/ppermute | solution.py:13
  328.1 18.4 %all-to-all-start = ((bf16[32,16,512]{2,0,1:T(8,128)(2,1)}), bf16[32,16,512]{2,0,1:T(8,128)(2,1)S(1)}, u32[]{:S(2)}, u32[]{:S(2)}) async-start(bf16[32,16,512]{2,0,1:T(8,128)(2,1)} %bitcast.109), calls=%async_computation | async-start | bytes 1048576 | tf_op jit(solution)/shard_map/while/body/eval_jaxpr/all_to_all | solution.py:101
  346.7 5.8 %collective-permute-start.1 = (bf16[32,512]{1,0:T(8,128)(2,1)S(1)}, bf16[32,512]{1,0:T(8,128)(2,1)S(1)}, u32[]{:S(2)}, u32[]{:S(2)}) collective-permute-start(bf16[32,512]{1,0:T(8,128)(2,1)S(1)} %fusion.38), channel_id=1, source_target_pairs={{16,0},{17,1},{18,2},{19,3},{20,4},{21,5},{22,6},{23,7},{24,8},{25... | collective-permute-start | bytes 98312 | tf_op jit(solution)/shard_map/while/body/eval_jaxpr/ppermute | solution.py:13
  359.3 18.4 %all-to-all-start = ((bf16[32,16,512]{2,0,1:T(8,128)(2,1)}), bf16[32,16,512]{2,0,1:T(8,128)(2,1)S(1)}, u32[]{:S(2)}, u32[]{:S(2)}) async-start(bf16[32,16,512]{2,0,1:T(8,128)(2,1)} %bitcast.109), calls=%async_computation | async-start | bytes 1048576 | tf_op jit(solution)/shard_map/while/body/eval_jaxpr/all_to_all | solution.py:101
  377.9 5.8 %collective-permute-start.1 = (bf16[32,512]{1,0:T(8,128)(2,1)S(1)}, bf16[32,512]{1,0:T(8,128)(2,1)S(1)}, u32[]{:S(2)}, u32[]{:S(2)}) collective-permute-start(bf16[32,512]{1,0:T(8,128)(2,1)S(1)} %fusion.38), channel_id=1, source_target_pairs={{16,0},{17,1},{18,2},{19,3},{20,4},{21,5},{22,6},{23,7},{24,8},{25... | collective-permute-start | bytes 98312 | tf_op jit(solution)/shard_map/while/body/eval_jaxpr/ppermute | solution.py:13
  390.5 18.4 %all-to-all-start = ((bf16[32,16,512]{2,0,1:T(8,128)(2,1)}), bf16[32,16,512]{2,0,1:T(8,128)(2,1)S(1)}, u32[]{:S(2)}, u32[]{:S(2)}) async-start(bf16[32,16,512]{2,0,1:T(8,128)(2,1)} %bitcast.109), calls=%async_computation | async-start | bytes 1048576 | tf_op jit(solution)/shard_map/while/body/eval_jaxpr/all_to_all | solution.py:101
  409.1 5.8 %collective-permute-start.1 = (bf16[32,512]{1,0:T(8,128)(2,1)S(1)}, bf16[32,512]{1,0:T(8,128)(2,1)S(1)}, u32[]{:S(2)}, u32[]{:S(2)}) collective-permute-start(bf16[32,512]{1,0:T(8,128)(2,1)S(1)} %fusion.38), channel_id=1, source_target_pairs={{16,0},{17,1},{18,2},{19,3},{20,4},{21,5},{22,6},{23,7},{24,8},{25... | collective-permute-start | bytes 98312 | tf_op jit(solution)/shard_map/while/body/eval_jaxpr/ppermute | solution.py:13
